TPU v7x, 32 devices: a whole 2x2x4 slice. The times are simulated.
32 devices in a mesh: dp: 4 (over y, x), vocab: 8 (over z, core).
Axes of the slice: x: 2, y: 2, z: 4, core: 2. Of those that a mesh axis runs over, the one named last changes fastest.
Arguments:
- hidden_states: bfloat16 [512, 3584], P('dp'), may hold values from -60 to 60
- unembed: bfloat16 [3584, 32768], P(None, ('dp', 'vocab')), may hold values from -0.3125 to 0.3125
- temp_code: int32 [512], P('dp'), may hold values from 20 to 200
- minp_code: int32 [512], P('dp'), may hold values from 1 to 30
Outputs:
- log_norm: float32 [512], P('dp')
- kept_mass: float32 [512], P('dp')
- kept_count: float32 [512], P('dp')
All inputs are finite; a program needn't handle non-finite values.
Results may differ from a plain program's by a relative error of at most 0.0003.
Values may be sent and summed in bfloat16 or wider, within the bound.
A program may use at most 64 MiB of HBM per device.

v0:
```python
import jax
import jax.numpy as jnp
from jax import lax
from jax.sharding import PartitionSpec as P


def finish(top_score, total, soft_count, retained_sum):
    return (top_score + jnp.log(total), retained_sum / total, jnp.log(1.0 + soft_count))


def on_device(hidden_states, unembed, temp_code, minp_code):
    raw_token_energy = jnp.dot(
        lax.all_gather(hidden_states, "dp", axis=0, tiled=True),
        unembed,
        preferred_element_type=jnp.float32,
    )
    own_logits = lax.all_to_all(raw_token_energy, "dp", split_axis=0, concat_axis=1, tiled=True)
    draw_softness_factor = temp_code.astype(jnp.float32) * 0.01
    min_prob = minp_code.astype(jnp.float32) * 0.01
    divided_token_energy = own_logits / draw_softness_factor[:, None]
    top_score = lax.pmax(jnp.max(divided_token_energy, axis=1), "vocab")
    exponent_values = jnp.exp(divided_token_energy - top_score[:, None])
    ramp = jnp.clip(
        1.0 + divided_token_energy - top_score[:, None] - jnp.log(min_prob)[:, None], 0.0, 1.0
    )
    total, soft_count, retained_sum = lax.psum(
        (
            jnp.sum(exponent_values, axis=1),
            jnp.sum(ramp, axis=1),
            jnp.sum(ramp * exponent_values, axis=1),
        ),
        "vocab",
    )
    return finish(top_score, total, soft_count, retained_sum)


def solution(mesh):
    in_specs = (P("dp", None), P(None, ("dp", "vocab")), P("dp"), P("dp"))
    out_specs = (P("dp"), P("dp"), P("dp"))
    return jax.shard_map(
        on_device, mesh=mesh, in_specs=in_specs, out_specs=out_specs, check_vma=False
    )
```

profile of v0, /device:TPU:0, one launch (start us, length us, event | category | flops | bytes accessed | tf_op | source)
XLA Modules:
  0.0 139.6 jit_solution(10602434122214719039)
XLA Ops:
  7.2 0.0 all-gather.2.cloned.1.call-start
  7.2 0.7 all-gather.2.cloned.1.call-update
  7.9 52.9 %all-gather.2.cloned.1.call-done = bf16[512,3584]{1,0:T(8,128)(2,1)} async-done(((bf16[128,3584]{1,0:T(8,128)(2,1)}), bf16[512,3584]{1,0:T(8,128)(2,1)}) %all-gather.2.cloned.1.call-update) | async-done | bytes 3670032 | tf_op jit(solution)/shard_map/all_gather | solution.py:13
  60.8 9.5 %fusion.4 = f32[512,1024]{1,0:T(8,128)} fusion(bf16[512,3584]{1,0:T(8,128)(2,1)} %all-gather.2.cloned.1.call-done, bf16[3584,1024]{1,0:T(8,128)(2,1)} %param.5), kind=kOutput, calls=%fused_computation.12 | convolution fusion | flops 3758096384 | bytes 13107200 | tf_op jit(solution)/shard_map/dot_general | solution.py:12
  70.3 0.0 copy-start
  70.3 0.0 copy-start.1
  70.3 3.7 %all-to-all-start = ((f32[4,128,1024]{2,1,0:T(8,128)}), f32[4,128,1024]{2,1,0:T(8,128)S(1)}, u32[]{:S(2)}, u32[]{:S(2)}) async-start(f32[4,128,1024]{2,1,0:T(8,128)} %bitcast.3), calls=%async_computation | async-start | bytes 4194304 | tf_op jit(solution)/shard_map/all_to_all | solution.py:17
  74.0 0.0 copy-done
  74.1 0.0 copy-done.1
  74.1 24.9 %all-to-all-done = f32[4,128,1024]{2,1,0:T(8,128)S(1)} async-done(((f32[4,128,1024]{2,1,0:T(8,128)}), f32[4,128,1024]{2,1,0:T(8,128)S(1)}, u32[]{:S(2)}, u32[]{:S(2)}) %all-to-all-start) | async-done | bytes 2097184 | tf_op jit(solution)/shard_map/all_to_all | solution.py:17
  99.0 1.6 %fusion.2 = (f32[128]{0:T(128)S(1)}, f32[4,128,1024]{2,1,0:T(8,128)}) fusion(f32[4,128,1024]{2,1,0:T(8,128)S(1)} %all-to-all-done, f32[128]{0:T(128)S(1)} %convert_multiply_fusion), kind=kLoop, calls=%fused_computation.10 | loop fusion | flops 1048448 | bytes 4195328 | tf_op jit(solution)/shard_map/reduce_max | solution.py:21
  100.6 15.6 %pmax.7 = f32[128]{0:T(128)S(1)} all-reduce(f32[128]{0:T(128)S(1)} %get-tuple-element.9), channel_id=1, replica_groups=mesh['dp'=4,'vocab'=8] {'vocab'}, use_global_device_ids=true, to_apply=%region_1.0 | all-reduce | flops 128 | bytes 1024 | tf_op jit(solution)/shard_map/pmax | solution.py:21
  116.1 2.5 %fusion.1 = (f32[128]{0:T(128)S(1)}, f32[128]{0:T(128)S(1)}, f32[128]{0:T(128)S(1)}) fusion(f32[4,128,1024]{2,1,0:T(8,128)} %get-tuple-element.10, f32[128]{0:T(128)S(1)} %multiply_log_fusion, f32[128]{0:T(128)S(1)} %pmax.7), kind=kLoop, calls=%fused_computation.4 | loop fusion | flops 4718208 | bytes 2099712 | tf_op jit(solution)/shard_map/reduce_sum | solution.py:29
  118.7 13.6 %all-reduce = (f32[128]{0:T(128)S(1)}, f32[128]{0:T(128)S(1)}, f32[128]{0:T(128)S(1)}) all-reduce(f32[128]{0:T(128)S(1)} %get-tuple-element.5, f32[128]{0:T(128)S(1)} %get-tuple-element.4, f32[128]{0:T(128)S(1)} %get-tuple-element.3), channel_id=1, replica_groups=mesh['dp'=4,'vocab'=8] {'vocab'}, use_global_device_ids=true, to_apply=%region_3.4 | all-reduce | flops 384 | bytes 3072 | tf_op jit(solution)/shard_map/psum | solution.py:26
  132.3 0.5 fusion.3
  (2 shorter events, 0.0 us)
Async XLA Ops:
  7.2 53.6 %all-gather.2.cloned.1.call-start = ((), (), s32[]{:S(2)}) async-start(), calls=%async_computation.1 | async-start | bytes 4587520 | tf_op jit(solution)/shard_map/all_gather | solution.py:13
  70.3 3.8 %copy-start = (s32[128]{0:T(128)S(1)}, s32[128]{0:T(128)}, u32[]{:S(2)}) copy-start(s32[128]{0:T(128)} %param.6) | copy-start | bytes 1540
  70.3 3.8 %copy-start.1 = (s32[128]{0:T(128)S(1)}, s32[128]{0:T(128)}, u32[]{:S(2)}) copy-start(s32[128]{0:T(128)} %param.7) | copy-start | bytes 1540
  70.3 28.7 %all-to-all-start = ((f32[4,128,1024]{2,1,0:T(8,128)}), f32[4,128,1024]{2,1,0:T(8,128)S(1)}, u32[]{:S(2)}, u32[]{:S(2)}) async-start(f32[4,128,1024]{2,1,0:T(8,128)} %bitcast.3), calls=%async_computation | async-start | bytes 4194304 | tf_op jit(solution)/shard_map/all_to_all | solution.py:17
Sparse Core Ops, SparseCore 0:
  9.8 50.9 all-gather.1
where the time goes:
time: 140 us
  waiting for transfers between devices  78.5 us (56%)
  blocking collectives  29.2 us (21%)
  between operations  14.1 us (10%)
  matrix products  9.49 us (7%)
  other arithmetic  4.66 us (3%)
  starting transfers between devices  3.78 us (3%)
    all_gather x1, waiting for transfers between devices, on_device(): lax.all_gather(hidden_states, 'dp', axis=0, tiled=True)  52.9 us
    all_to_all x1, waiting for transfers between devices, on_device(): lax.all_to_all(raw_token_energy, 'dp', split_axis=0, concat_axis=1, tiled...  24.9 us
    pmax x1, blocking collectives, on_device(): top_score = lax.pmax(jnp.max(divided_token_energy, axis=1), 'vocab')  15.6 us
    psum x1, blocking collectives, on_device(): lax.psum((jnp.sum(exponent_values, axis=1), jnp.sum(ramp, axis=1), jnp.su...  13.6 us
    dot_general x1, matrix products, on_device(): jnp.dot(lax.all_gather(hidden_states, 'dp', axis=0, tiled=True), unembed,...  9.49 us
    all_to_all x1, starting transfers between devices, on_device(): lax.all_to_all(raw_token_energy, 'dp', split_axis=0, concat_axis=1, tiled...  3.74 us
  transfers between devices with their start and end apart: 2, of which 2 were waited for; matrix products, arithmetic and copies ran while one was open for 0% of the time, Pallas kernels for 0%

commit v1 on v0

v1 whole, which is shorter than its diff:
```python
import functools

import jax
import jax.numpy as jnp
from jax import lax
from jax.experimental import pallas as pl
from jax.experimental.pallas import tpu as pltpu
from jax.sharding import PartitionSpec as P

MESH = pl.DeviceIdType.MESH
LANES = 128
PIECE = 16
WIDE = 256


def flip(index, bit):
    return index + bit * (1 - 2 * ((index // bit) % 2))


def kernel(
    n_dp, n_vocab,
    h_ref, w_ref, temp_ref, minp_ref,
    norm_ref, mass_ref, count_ref,
    own, weights, gathered, logits, codes_t, codes_p, inv_col, base_col, sums,
    top_col, tops, max_box, part, sum_box,
    own_sem, w_sem, ici_send, ici_recv, core_send, core_recv,
    code_send, code_recv, max_send, max_recv, sum_send, sum_recv,
):
    d = lax.axis_index("dp")
    v = lax.axis_index("vocab")
    n_all = n_dp * n_vocab
    me = d * n_vocab + v
    core = v % 2
    rows, depth = h_ref.shape
    vocab = w_ref.shape[1]
    n_roles = n_dp - 1
    n_chunks = rows // (2 * PIECE)
    chunk_rows = 2 * PIECE
    relayed = n_dp == 4

    if relayed:
        parity = (v // 2) % 2
        first = (1 - parity) * flip(d, 1) + parity * flip(d, 2)
        second = (1 - parity) * flip(d, 2) + parity * flip(d, 1)
        blocks = [first, flip(flip(d, 1), 2), second]
        targets = [(first, v), (second, v), (d, flip(v, 2))]
    else:
        blocks = [(d + n_dp - 1 - r) % n_dp for r in range(n_roles)]
        targets = [((d + 1 + r) % n_dp, v) for r in range(n_roles)]
    partner = (d, flip(v, 1))

    n_w = w_sem.shape[0]
    w_step = depth // n_w
    own_copy = pltpu.make_async_copy(h_ref, own, own_sem)
    own_copy.start()
    w_copies = []
    for i in range(n_w):
        part_of = pl.ds(i * w_step, w_step)
        w_copies.append(pltpu.make_async_copy(w_ref.at[part_of], weights.at[part_of], w_sem.at[i]))
        w_copies[-1].start()

    barrier = pltpu.get_barrier_semaphore()

    @pl.loop(1, n_all)
    def _(j):
        t = (me + j) % n_all
        pl.semaphore_signal(barrier, inc=1, device_id=(t // n_vocab, t % n_vocab), device_id_type=MESH)

    pl.semaphore_wait(barrier, n_all - 1)

    code_copies = []
    for r in range(n_roles):
        to = ((d + 1 + r) % n_dp, v)
        for s, (src, dst) in enumerate(((temp_ref, codes_t), (minp_ref, codes_p))):
            code_copies.append(pltpu.make_async_remote_copy(
                src_ref=src, dst_ref=dst.at[r], send_sem=code_send.at[s, r],
                recv_sem=code_recv.at[s, r], device_id=to, device_id_type=MESH))

    own_copy.wait()

    def own_piece(i):
        return own.at[pl.ds(pl.multiple_of(i * chunk_rows + core * PIECE, PIECE), PIECE)]

    def slot(i, r):
        return gathered.at[i, r, core]

    def send(src, i, r, sem):
        return pltpu.make_async_remote_copy(
            src_ref=src, dst_ref=slot(i, r), send_sem=sem, recv_sem=ici_recv.at[r, i],
            device_id=targets[r], device_id_type=MESH)

    def to_partner(i, r):
        return pltpu.make_async_remote_copy(
            src_ref=slot(i, r), dst_ref=slot(i, r), send_sem=core_send.at[r, i],
            recv_sem=core_recv.at[r, i], device_id=partner, device_id_type=MESH)

    direct = [0] if relayed else list(range(n_roles))
    sends = {}
    for i in range(n_chunks):
        for r in range(n_roles):
            src = own_piece(i) if r in direct else slot(i, 0)
            sends[r, i] = send(src, i, r, ici_send.at[r, i])
    passes = {(r, i): to_partner(i, r) for r in range(n_roles) for i in range(n_chunks)}
    for i in range(n_chunks):
        for r in direct:
            sends[r, i].start()
    for c in code_copies:
        c.start()

    def local_max(values):
        return functools.reduce(jnp.maximum, [values[:, t * LANES:(t + 1) * LANES] for t in range(WIDE // LANES)])

    def to_row(values, op):
        return op(values.T, axis=0, keepdims=True)

    for c in w_copies:
        c.wait()

    def own_step(n, best):
        cols = pl.ds(pl.multiple_of(n * WIDE, WIDE), WIDE)
        out = jnp.dot(own[...], weights[:, cols], preferred_element_type=jnp.float32)
        logits[0, :, cols] = out
        return jnp.maximum(best, local_max(out))

    best = lax.fori_loop(0, vocab // WIDE, own_step, jnp.full((rows, LANES), -jnp.inf, jnp.float32))
    max_box[0, pl.ds(d, 1), :] = to_row(best, jnp.max)

    def column(row):
        return jnp.broadcast_to(row, (LANES, LANES)).T

    def keep_columns(r, temp, minp):
        inv_col[r] = column(1.0 / (temp.astype(jnp.float32) * 0.01))
        base_col[r] = column(1.0 - jnp.log(minp.astype(jnp.float32) * 0.01))

    keep_columns(0, temp_ref[...], minp_ref[...])

    group = max(n_chunks // 2, 1)
    for g in range(n_chunks // group):
        chunks = range(g * group, (g + 1) * group)
        for i in chunks:
            for r in direct:
                sends[r, i].wait_recv()
                if relayed:
                    sends[1, i].start()
                    sends[2, i].start()
                passes[r, i].start()
        for i in chunks:
            for r in range(n_roles):
                if r not in direct:
                    sends[r, i].wait_recv()
                    passes[r, i].start()
        if g == 0:
            for c in code_copies:
                c.wait()
            for r in range(n_roles):
                s = ((d + n_dp - blocks[r]) % n_dp) - 1
                keep_columns(r + 1, codes_t[s], codes_p[s])
        for i in chunks:
            for r in range(n_roles):
                passes[r, i].wait_recv()
        many = group * n_roles * chunk_rows

        def step(n, best):
            cols = pl.ds(pl.multiple_of(n * WIDE, WIDE), WIDE)
            lhs = gathered[g * group:(g + 1) * group].reshape(many, depth)
            out = jnp.dot(lhs, weights[:, cols], preferred_element_type=jnp.float32)
            for a, i in enumerate(chunks):
                for r in range(n_roles):
                    at = (a * n_roles + r) * chunk_rows
                    logits[r + 1, i * chunk_rows:(i + 1) * chunk_rows, cols] = out[at:at + chunk_rows]
            return jnp.maximum(best, local_max(out))

        best = lax.fori_loop(0, vocab // WIDE, step, jnp.full((many, LANES), -jnp.inf, jnp.float32))
        for r in range(n_roles):
            rows_r = [best[(a * n_roles + r) * chunk_rows:(a * n_roles + r + 1) * chunk_rows] for a in range(group)]
            piece = jnp.concatenate(rows_r, axis=0)
            wide = group * chunk_rows
            max_box[0, pl.ds(blocks[r], 1), g * wide:(g + 1) * wide] = to_row(piece, jnp.max)

    def exchange(source, box, send_sem, recv_sem):
        def copy(j):
            t = (me + j) % n_all
            return pltpu.make_async_remote_copy(
                src_ref=source(t // n_vocab), dst_ref=box.at[j], send_sem=send_sem, recv_sem=recv_sem,
                device_id=(t // n_vocab, t % n_vocab), device_id_type=MESH)

        @pl.loop(1, n_all)
        def _(j):
            copy(j).start()

        rest = box.at[pl.ds(1, n_all - 1)]
        return pltpu.make_async_copy(rest, rest, send_sem), pltpu.make_async_copy(rest, rest, recv_sem)

    max_sent, max_got = exchange(lambda block: max_box.at[0], max_box, max_send, max_recv)
    max_got.wait()
    tops[...] = jnp.max(max_box[...], axis=0)
    max_sent.wait()

    lane_tiles = vocab // LANES
    strip = 32
    for r in range(n_dp):
        block = d if r == 0 else blocks[r - 1]
        top_col[...] = column(tops[pl.ds(block, 1), :])

        @pl.loop(0, rows // strip)
        def _(q):
            at = pl.ds(pl.multiple_of(q * strip, strip), strip)
            top, inv, base = top_col[at], inv_col[r, at], base_col[r, at]
            total = count = mass = jnp.zeros((strip, LANES), jnp.float32)
            for t in range(lane_tiles):
                below = (logits[r, at, t * LANES:(t + 1) * LANES] - top) * inv
                term = jnp.exp(below)
                ramp = jnp.clip(below + base, 0.0, 1.0)
                total, count, mass = total + term, count + ramp, mass + ramp * term
            sums[0, at], sums[1, at], sums[2, at] = total, count, mass

        rows_of = [to_row(sums[s], jnp.sum) for s in range(3)]
        part[pl.ds(block, 1)] = jnp.concatenate(rows_of + [jnp.zeros_like(rows_of[0])], axis=0)[None]

    sum_box[0] = part[d]
    sum_sent, sum_got = exchange(lambda block: part.at[block], sum_box, sum_send, sum_recv)
    temperature = temp_ref[...].astype(jnp.float32) * 0.01
    top_score = tops[pl.ds(d, 1), :] / temperature
    sum_got.wait()
    whole = jnp.sum(sum_box[...], axis=0)
    total, count, mass = whole[0:1], whole[1:2], whole[2:3]
    norm_ref[...] = top_score + jnp.log(total)
    mass_ref[...] = mass / total
    count_ref[...] = jnp.log(1.0 + count)

    sum_sent.wait()
    for c in (*sends.values(), *passes.values()):
        c.wait_send()


def on_device(n_dp, n_vocab, hidden_states, unembed, temp_code, minp_code):
    rows, depth = hidden_states.shape
    vocab = unembed.shape[1]
    n_all = n_dp * n_vocab
    n_roles = n_dp - 1
    n_chunks = rows // (2 * PIECE)
    f32, i32, bf16 = jnp.float32, jnp.int32, hidden_states.dtype
    dma = pltpu.SemaphoreType.DMA
    vmem = pl.BlockSpec(memory_space=pltpu.VMEM)
    any_space = pl.BlockSpec(memory_space=pl.ANY)
    outs = pl.pallas_call(
        functools.partial(kernel, n_dp, n_vocab),
        out_shape=[jax.ShapeDtypeStruct((1, rows), f32)] * 3,
        in_specs=[any_space, any_space, vmem, vmem],
        out_specs=[vmem] * 3,
        scratch_shapes=[
            pltpu.VMEM((rows, depth), bf16),
            pltpu.VMEM((depth, vocab), bf16),
            pltpu.VMEM((n_chunks, n_roles, 2, PIECE, depth), bf16),
            pltpu.VMEM((n_dp, rows, vocab), f32),
            pltpu.VMEM((n_roles, 1, rows), i32),
            pltpu.VMEM((n_roles, 1, rows), i32),
            pltpu.VMEM((n_dp, rows, LANES), f32),
            pltpu.VMEM((n_dp, rows, LANES), f32),
            pltpu.VMEM((3, rows, LANES), f32),
            pltpu.VMEM((rows, LANES), f32),
            pltpu.VMEM((n_dp, rows), f32),
            pltpu.VMEM((n_all, n_dp, rows), f32),
            pltpu.VMEM((n_dp, 4, rows), f32),
            pltpu.VMEM((n_all, 4, rows), f32),
            dma, dma((4,)),
            dma((n_roles, n_chunks)), dma((n_roles, n_chunks)),
            dma((n_roles, n_chunks)), dma((n_roles, n_chunks)),
            dma((2, n_roles)), dma((2, n_roles)),
            dma, dma, dma, dma,
        ],
        compiler_params=pltpu.CompilerParams(collective_id=0, has_side_effects=True),
    )(hidden_states, unembed, temp_code.reshape(1, rows), minp_code.reshape(1, rows))
    return tuple(o.reshape(rows) for o in outs)


def solution(mesh):
    in_specs = (P("dp", None), P(None, ("dp", "vocab")), P("dp"), P("dp"))
    out_specs = (P("dp"), P("dp"), P("dp"))
    body = functools.partial(on_device, mesh.shape["dp"], mesh.shape["vocab"])
    return jax.shard_map(body, mesh=mesh, in_specs=in_specs, out_specs=out_specs, check_vma=False)
```

time: 140 us -> 49.2 us (0.35)
  waiting for transfers between devices: 78.5 us -> 0 us
  Pallas kernels: 0 us -> 44.9 us
  blocking collectives: 29.2 us -> 0 us
  between operations: 14.1 us -> 0.64 us
  matrix products: 9.49 us -> 0 us
  other arithmetic: 4.66 us -> 0 us
  starting transfers between devices: 3.78 us -> 0 us
  local copies, waits for them, and re-layouts: 0.01 us -> 3.42 us
    all_gather x1 -> x0, waiting for transfers between devices: 52.9 us -> none  [on_device(): lax.all_gather(hidden_states, 'dp', axis=0, tiled=True)]
    pallas_call x0 -> x1, Pallas kernels: none -> 44.9 us  [on_device(): pl.pallas_call(functools.partial(kernel, n_dp, n_vocab), out_shape=[jax.S...]
    all_to_all x1 -> x0, waiting for transfers between devices: 24.9 us -> none  [on_device(): lax.all_to_all(raw_token_energy, 'dp', split_axis=0, concat_axis=1, tiled...]
    pmax x1 -> x0, blocking collectives: 15.6 us -> none  [on_device(): top_score = lax.pmax(jnp.max(divided_token_energy, axis=1), 'vocab')]
    psum x1 -> x0, blocking collectives: 13.6 us -> none  [on_device(): lax.psum((jnp.sum(exponent_values, axis=1), jnp.sum(ramp, axis=1), jnp.su...]
    dot_general x1 -> x0, matrix products: 9.49 us -> none  [on_device(): jnp.dot(lax.all_gather(hidden_states, 'dp', axis=0, tiled=True), unembed,...]
    all_to_all x1 -> x0, starting transfers between devices: 3.74 us -> none  [on_device(): lax.all_to_all(raw_token_energy, 'dp', split_axis=0, concat_axis=1, tiled...]
    unnamed x4 -> x3, local copies, waits for them, and re-layouts: 0.01 us -> 3.42 us
  transfers between devices with their start and end apart: 2 -> 0, of which waited for: 2 -> 0; matrix products, arithmetic and copies ran while one was open for 0% -> 0% of each run, Pallas kernels for 0% -> 0%
where the time goes in v1:
time: 49.2 us; the launch traced here: 49 us
  Pallas kernels  44.9 us (91%)
  local copies, waits for them, and re-layouts  3.42 us (7%)
  between operations  0.64 us (1%)
    pallas_call x1, Pallas kernels, on_device(): pl.pallas_call(functools.partial(kernel, n_dp, n_vocab), out_shape=[jax.S...  44.9 us
    unnamed x3, local copies, waits for them, and re-layouts  3.42 us

profile of v1, /device:TPU:0, one launch (start us, length us, event | category | flops | bytes accessed | tf_op | source)
XLA Modules:
  0.0 49.0 jit_solution(12830875754644053054)
XLA Ops:
  0.6 44.9 %shard_map.67 = (f32[1,128]{1,0:T(1,128)}, f32[1,128]{1,0:T(1,128)}, f32[1,128]{1,0:T(1,128)}) custom-call(bf16[128,3584]{1,0:T(8,128)(2,1)} %h_ref.1, bf16[3584,1024]{1,0:T(8,128)(2,1)} %w_ref.1, s32[1,128]{1,0:T(1,128)} %bitcast.5, s32[1,128]{1,0:T(1,128)} %bitcast.6), custom_call_target="tpu_custom_call" | custom-call | tf_op jit(solution)/shard_map/pallas_call | solution.py:246
  45.5 1.1 %copy.10 = f32[128]{0:T(128)} copy(f32[128]{0:T(128)} %bitcast.9) | data formatting | bytes 1024
  46.7 1.1 %copy.11 = f32[128]{0:T(128)} copy(f32[128]{0:T(128)} %bitcast.8) | data formatting | bytes 1024
  47.8 1.2 %copy.12 = f32[128]{0:T(128)} copy(f32[128]{0:T(128)} %bitcast.7) | data formatting | bytes 1024

commit v2 on v1

--- a/solution.py
+++ b/solution.py
@@ -10,6 +10,7 @@
 MESH = pl.DeviceIdType.MESH
 LANES = 128
 PIECE = 16
+SPLIT = 2
 WIDE = 256
 
 
@@ -20,11 +21,11 @@
 def kernel(
     n_dp, n_vocab,
     h_ref, w_ref, temp_ref, minp_ref,
-    norm_ref, mass_ref, count_ref,
+    out_ref,
     own, weights, gathered, logits, codes_t, codes_p, inv_col, base_col, sums,
     top_col, tops, max_box, part, sum_box,
     own_sem, w_sem, ici_send, ici_recv, core_send, core_recv,
-    code_send, code_recv, max_send, max_recv, sum_send, sum_recv,
+    code_send, code_recv, max_send, max_recv, sum_send, sum_recv, seen,
 ):
     d = lax.axis_index("dp")
     v = lax.axis_index("vocab")
@@ -44,9 +45,11 @@
         second = (1 - parity) * flip(d, 2) + parity * flip(d, 1)
         blocks = [first, flip(flip(d, 1), 2), second]
         targets = [(first, v), (second, v), (d, flip(v, 2))]
+        near = [[(flip(d, 1), v)], [(flip(d, 2), v)]]
     else:
         blocks = [(d + n_dp - 1 - r) % n_dp for r in range(n_roles)]
         targets = [((d + 1 + r) % n_dp, v) for r in range(n_roles)]
+        near = [targets]
     partner = (d, flip(v, 1))
 
     n_w = w_sem.shape[0]
@@ -57,16 +60,50 @@
     for i in range(n_w):
         part_of = pl.ds(i * w_step, w_step)
         w_copies.append(pltpu.make_async_copy(w_ref.at[part_of], weights.at[part_of], w_sem.at[i]))
-        w_copies[-1].start()
 
     barrier = pltpu.get_barrier_semaphore()
-
-    @pl.loop(1, n_all)
-    def _(j):
-        t = (me + j) % n_all
-        pl.semaphore_signal(barrier, inc=1, device_id=(t // n_vocab, t % n_vocab), device_id_type=MESH)
-
-    pl.semaphore_wait(barrier, n_all - 1)
+    line = v // 2
+    has_low = line > 0
+    has_high = line < n_vocab // 2 - 1
+    ends = has_low.astype(jnp.int32) + has_high.astype(jnp.int32)
+
+    def signal(sem, to):
+        pl.semaphore_signal(sem, inc=1, device_id=to, device_id_type=MESH)
+
+    def signal_line(sem):
+        @pl.when(has_low)
+        def _():
+            signal(sem, (d, v - 2))
+
+        @pl.when(has_high)
+        def _():
+            signal(sem, (d, v + 2))
+
+    direct_peers = [to for stage in near for to in stage] + [partner]
+    for to in direct_peers:
+        signal(barrier, to)
+    signal_line(barrier)
+    for c in w_copies:
+        c.start()
+    pl.semaphore_wait(barrier, len(direct_peers) + ends)
+
+    def line_round(k):
+        def run():
+            signal_line(seen.at[k])
+            pl.semaphore_wait(seen.at[k], ends)
+        return run
+
+    def peer_round(k, peers):
+        def run():
+            for to in peers:
+                signal(seen.at[k], to)
+            pl.semaphore_wait(seen.at[k], len(peers))
+        return run
+
+    n_line = n_vocab // 2 - 2
+    chores = [line_round(k) for k in range(n_line)]
+    for k, peers in enumerate(near + [[partner]]):
+        chores.append(peer_round(n_line + k, peers))
 
     code_copies = []
     for r in range(n_roles):
@@ -76,36 +113,61 @@
                 src_ref=src, dst_ref=dst.at[r], send_sem=code_send.at[s, r],
                 recv_sem=code_recv.at[s, r], device_id=to, device_id_type=MESH))
 
+    def start_codes():
+        for c in code_copies:
+            c.start()
+
+    chores.append(start_codes)
+
+    def chore(count=1):
+        for _ in range(min(count, len(chores))):
+            chores.pop(0)()
+
+    n_units = n_chunks * SPLIT
+    width = depth // SPLIT
+
+    def own_piece(u):
+        at = pl.multiple_of((u // SPLIT) * chunk_rows + core * PIECE, PIECE)
+        return own.at[pl.ds(at, PIECE), pl.ds((u % SPLIT) * width, width)]
+
+    def slot(u, r):
+        return gathered.at[u // SPLIT, r, core, :, pl.ds((u % SPLIT) * width, width)]
+
+    def send(src, u, r, sem):
+        return pltpu.make_async_remote_copy(
+            src_ref=src, dst_ref=slot(u, r), send_sem=sem, recv_sem=ici_recv.at[r, u],
+            device_id=targets[r], device_id_type=MESH)
+
+    def to_partner(u, r):
+        return pltpu.make_async_remote_copy(
+            src_ref=slot(u, r), dst_ref=slot(u, r), send_sem=core_send.at[r, u],
+            recv_sem=core_recv.at[r, u], device_id=partner, device_id_type=MESH)
+
+    direct = [0] if relayed else list(range(n_roles))
+    others = [r for r in range(n_roles) if r not in direct]
+    sends = {}
+    for u in range(n_units):
+        for r in range(n_roles):
+            src = own_piece(u) if r in direct else slot(u, 0)
+            sends[r, u] = send(src, u, r, ici_send.at[r, u])
+    passes = {(r, u): to_partner(u, r) for r in range(n_roles) for u in range(n_units)}
     own_copy.wait()
-
-    def own_piece(i):
-        return own.at[pl.ds(pl.multiple_of(i * chunk_rows + core * PIECE, PIECE), PIECE)]
-
-    def slot(i, r):
-        return gathered.at[i, r, core]
-
-    def send(src, i, r, sem):
-        return pltpu.make_async_remote_copy(
-            src_ref=src, dst_ref=slot(i, r), send_sem=sem, recv_sem=ici_recv.at[r, i],
-            device_id=targets[r], device_id_type=MESH)
-
-    def to_partner(i, r):
-        return pltpu.make_async_remote_copy(
-            src_ref=slot(i, r), dst_ref=slot(i, r), send_sem=core_send.at[r, i],
-            recv_sem=core_recv.at[r, i], device_id=partner, device_id_type=MESH)
-
-    direct = [0] if relayed else list(range(n_roles))
-    sends = {}
-    for i in range(n_chunks):
-        for r in range(n_roles):
-            src = own_piece(i) if r in direct else slot(i, 0)
-            sends[r, i] = send(src, i, r, ici_send.at[r, i])
-    passes = {(r, i): to_partner(i, r) for r in range(n_roles) for i in range(n_chunks)}
-    for i in range(n_chunks):
+    for u in range(n_units):
         for r in direct:
-            sends[r, i].start()
-    for c in code_copies:
-        c.start()
+            sends[r, u].start()
+    chore()
+
+    def take_direct(u):
+        for r in direct:
+            sends[r, u].wait_recv()
+            for o in others:
+                sends[o, u].start()
+            passes[r, u].start()
+
+    def take_others(u):
+        for r in others:
+            sends[r, u].wait_recv()
+            passes[r, u].start()
 
     def local_max(values):
         return functools.reduce(jnp.maximum, [values[:, t * LANES:(t + 1) * LANES] for t in range(WIDE // LANES)])
@@ -113,6 +175,7 @@
     def to_row(values, op):
         return op(values.T, axis=0, keepdims=True)
 
+    take_direct(0)
     for c in w_copies:
         c.wait()
 
@@ -134,35 +197,30 @@
 
     keep_columns(0, temp_ref[...], minp_ref[...])
 
-    group = max(n_chunks // 2, 1)
-    for g in range(n_chunks // group):
-        chunks = range(g * group, (g + 1) * group)
-        for i in chunks:
-            for r in direct:
-                sends[r, i].wait_recv()
-                if relayed:
-                    sends[1, i].start()
-                    sends[2, i].start()
-                passes[r, i].start()
-        for i in chunks:
-            for r in range(n_roles):
-                if r not in direct:
-                    sends[r, i].wait_recv()
-                    passes[r, i].start()
-        if g == 0:
+    for u in range(1, n_units):
+        take_direct(u)
+        chore()
+        take_others(u - 1)
+    chore(len(chores))
+
+    for chunks in (range(n_chunks - 1), range(n_chunks - 1, n_chunks)):
+        g, group = chunks[0], len(chunks)
+        if g:
+            take_others(n_units - 1)
+        else:
             for c in code_copies:
                 c.wait()
             for r in range(n_roles):
                 s = ((d + n_dp - blocks[r]) % n_dp) - 1
                 keep_columns(r + 1, codes_t[s], codes_p[s])
-        for i in chunks:
+        for u in range(g * SPLIT, (g + group) * SPLIT):
             for r in range(n_roles):
-                passes[r, i].wait_recv()
+                passes[r, u].wait_recv()
         many = group * n_roles * chunk_rows
 
         def step(n, best):
             cols = pl.ds(pl.multiple_of(n * WIDE, WIDE), WIDE)
-            lhs = gathered[g * group:(g + 1) * group].reshape(many, depth)
+            lhs = gathered[g:g + group].reshape(many, depth)
             out = jnp.dot(lhs, weights[:, cols], preferred_element_type=jnp.float32)
             for a, i in enumerate(chunks):
                 for r in range(n_roles):
@@ -174,19 +232,23 @@
         for r in range(n_roles):
             rows_r = [best[(a * n_roles + r) * chunk_rows:(a * n_roles + r + 1) * chunk_rows] for a in range(group)]
             piece = jnp.concatenate(rows_r, axis=0)
-            wide = group * chunk_rows
-            max_box[0, pl.ds(blocks[r], 1), g * wide:(g + 1) * wide] = to_row(piece, jnp.max)
+            max_box[0, pl.ds(blocks[r], 1), g * chunk_rows:(g + group) * chunk_rows] = to_row(piece, jnp.max)
 
     def exchange(source, box, send_sem, recv_sem):
-        def copy(j):
-            t = (me + j) % n_all
-            return pltpu.make_async_remote_copy(
-                src_ref=source(t // n_vocab), dst_ref=box.at[j], send_sem=send_sem, recv_sem=recv_sem,
-                device_id=(t // n_vocab, t % n_vocab), device_id_type=MESH)
-
-        @pl.loop(1, n_all)
-        def _(j):
-            copy(j).start()
+        def send_row(down, skip):
+            to_d = (d + down) % n_dp
+            for across in reversed(range(skip, n_vocab)):
+                pltpu.make_async_remote_copy(
+                    src_ref=source(to_d), dst_ref=box.at[down * n_vocab + across],
+                    send_sem=send_sem, recv_sem=recv_sem,
+                    device_id=(to_d, (v + across) % n_vocab), device_id_type=MESH).start()
+
+        if n_dp > 4:
+            pl.loop(1, n_dp)(lambda down: send_row(down, 0))
+        else:
+            for down in range(1, n_dp):
+                send_row(down, 0)
+        send_row(0, 1)
 
         rest = box.at[pl.ds(1, n_all - 1)]
         return pltpu.make_async_copy(rest, rest, send_sem), pltpu.make_async_copy(rest, rest, recv_sem)
@@ -224,9 +286,9 @@
     sum_got.wait()
     whole = jnp.sum(sum_box[...], axis=0)
     total, count, mass = whole[0:1], whole[1:2], whole[2:3]
-    norm_ref[...] = top_score + jnp.log(total)
-    mass_ref[...] = mass / total
-    count_ref[...] = jnp.log(1.0 + count)
+    out_ref[0:1] = top_score + jnp.log(total)
+    out_ref[1:2] = mass / total
+    out_ref[2:3] = jnp.log(1.0 + count)
 
     sum_sent.wait()
     for c in (*sends.values(), *passes.values()):
@@ -245,9 +307,9 @@
     any_space = pl.BlockSpec(memory_space=pl.ANY)
     outs = pl.pallas_call(
         functools.partial(kernel, n_dp, n_vocab),
-        out_shape=[jax.ShapeDtypeStruct((1, rows), f32)] * 3,
+        out_shape=jax.ShapeDtypeStruct((3, rows), f32),
         in_specs=[any_space, any_space, vmem, vmem],
-        out_specs=[vmem] * 3,
+        out_specs=vmem,
         scratch_shapes=[
             pltpu.VMEM((rows, depth), bf16),
             pltpu.VMEM((depth, vocab), bf16),
@@ -264,14 +326,14 @@
             pltpu.VMEM((n_dp, 4, rows), f32),
             pltpu.VMEM((n_all, 4, rows), f32),
             dma, dma((4,)),
-            dma((n_roles, n_chunks)), dma((n_roles, n_chunks)),
-            dma((n_roles, n_chunks)), dma((n_roles, n_chunks)),
+            *[dma((n_roles, n_chunks * SPLIT))] * 4,
             dma((2, n_roles)), dma((2, n_roles)),
             dma, dma, dma, dma,
+            pltpu.SemaphoreType.REGULAR((n_vocab // 2 + 1,)),
         ],
         compiler_params=pltpu.CompilerParams(collective_id=0, has_side_effects=True),
     )(hidden_states, unembed, temp_code.reshape(1, rows), minp_code.reshape(1, rows))
-    return tuple(o.reshape(rows) for o in outs)
+    return outs[0], outs[1], outs[2]
 
 
 def solution(mesh):

time: 49.2 us -> 43.6 us (0.89)
  Pallas kernels: 44.9 us -> 41.4 us
  local copies, waits for them, and re-layouts: 3.42 us -> 1.3 us
    pallas_call x1, Pallas kernels: 44.9 us -> 41.4 us  [on_device(): pl.pallas_call(functools.partial(kernel, n_dp, n_vocab), out_shape=jax.Sh...]
    unnamed x3 -> x0, local copies, waits for them, and re-layouts: 3.42 us -> none
    squeeze x0 -> x1, local copies, waits for them, and re-layouts: none -> 1.3 us  [on_device(): return (outs[0], outs[1], outs[2])]
where the time goes in v2:
time: 43.6 us; the launch traced here: 43.4 us
  Pallas kernels  41.4 us (95%)
  local copies, waits for them, and re-layouts  1.3 us (3%)
  between operations  0.64 us (1%)
    pallas_call x1, Pallas kernels, on_device(): pl.pallas_call(functools.partial(kernel, n_dp, n_vocab), out_shape=jax.Sh...  41.4 us
    squeeze x1, local copies, waits for them, and re-layouts, on_device(): return (outs[0], outs[1], outs[2])  1.3 us

profile of v2, /device:TPU:0, one launch (start us, length us, event | category | flops | bytes accessed | tf_op | source)
XLA Modules:
  0.0 43.4 jit_solution(15152796762688663970)
XLA Ops:
  0.6 41.4 %shard_map.67 = f32[3,128]{1,0:T(4,128)} custom-call(bf16[128,3584]{1,0:T(8,128)(2,1)} %h_ref.1, bf16[3584,1024]{1,0:T(8,128)(2,1)} %w_ref.1, s32[1,128]{1,0:T(1,128)} %bitcast.8, s32[1,128]{1,0:T(1,128)} %bitcast.9), custom_call_target="tpu_custom_call" | custom-call | tf_op jit(solution)/shard_map/pallas_call | solution.py:308
  42.1 1.3 %slice_bitcast_fusion = (f32[128]{0:T(128)}, f32[128]{0:T(128)}, f32[128]{0:T(128)}) fusion(f32[3,128]{1,0:T(4,128)} %shard_map.67), kind=kLoop, calls=%fused_computation | loop fusion | bytes 3072 | tf_op jit(solution)/shard_map/squeeze | solution.py:336

commit v3 on v2

--- a/solution.py
+++ b/solution.py
@@ -10,7 +10,7 @@
 MESH = pl.DeviceIdType.MESH
 LANES = 128
 PIECE = 16
-SPLIT = 2
+SPLIT = 1
 WIDE = 256
 
 
@@ -197,17 +197,20 @@
 
     keep_columns(0, temp_ref[...], minp_ref[...])
 
+    early = max(n_chunks - 2, 1)
     for u in range(1, n_units):
         take_direct(u)
         chore()
-        take_others(u - 1)
+        if u <= early * SPLIT:
+            take_others(u - 1)
     chore(len(chores))
 
-    for chunks in (range(n_chunks - 1), range(n_chunks - 1, n_chunks)):
+    for chunks in [range(early)] + [range(i, i + 1) for i in range(early, n_chunks)]:
         g, group = chunks[0], len(chunks)
         if g:
-            take_others(n_units - 1)
-        else:
+            for u in range(g * SPLIT, (g + 1) * SPLIT):
+                take_others(u)
+        if g == early:
             for c in code_copies:
                 c.wait()
             for r in range(n_roles):

time: 43.6 us -> 41.5 us (0.952)
  Pallas kernels: 41.4 us -> 39.4 us
    pallas_call x1, Pallas kernels: 41.4 us -> 39.4 us  [on_device(): pl.pallas_call(functools.partial(kernel, n_dp, n_vocab), out_shape=jax.Sh...]
where the time goes in v3:
time: 41.5 us; the launch traced here: 41.3 us
  Pallas kernels  39.4 us (95%)
  local copies, waits for them, and re-layouts  1.3 us (3%)
  between operations  0.64 us (2%)
    pallas_call x1, Pallas kernels, on_device(): pl.pallas_call(functools.partial(kernel, n_dp, n_vocab), out_shape=jax.Sh...  39.4 us
    squeeze x1, local copies, waits for them, and re-layouts, on_device(): return (outs[0], outs[1], outs[2])  1.3 us

profile of v3, /device:TPU:0, one launch (start us, length us, event | category | flops | bytes accessed | tf_op | source)
XLA Modules:
  0.0 41.3 jit_solution(2012809167711738646)
XLA Ops:
  0.6 39.4 %shard_map.67 = f32[3,128]{1,0:T(4,128)} custom-call(bf16[128,3584]{1,0:T(8,128)(2,1)} %h_ref.1, bf16[3584,1024]{1,0:T(8,128)(2,1)} %w_ref.1, s32[1,128]{1,0:T(1,128)} %bitcast.8, s32[1,128]{1,0:T(1,128)} %bitcast.9), custom_call_target="tpu_custom_call" | custom-call | tf_op jit(solution)/shard_map/pallas_call | solution.py:311
  40.0 1.3 %slice_bitcast_fusion = (f32[128]{0:T(128)}, f32[128]{0:T(128)}, f32[128]{0:T(128)}) fusion(f32[3,128]{1,0:T(4,128)} %shard_map.67), kind=kLoop, calls=%fused_computation | loop fusion | bytes 3072 | tf_op jit(solution)/shard_map/squeeze | solution.py:339

commit v4 on v3

--- a/solution.py
+++ b/solution.py
@@ -155,7 +155,7 @@
     for u in range(n_units):
         for r in direct:
             sends[r, u].start()
-    chore()
+    chore(3)
 
     def take_direct(u):
         for r in direct:

time: 41.5 us -> 41.2 us (level)
  no operation moved by 1% of the time
where the time goes in v4:
time: 41.2 us; the launch traced here: 41 us
  Pallas kernels  39.1 us (95%)
  local copies, waits for them, and re-layouts  1.3 us (3%)
  between operations  0.64 us (2%)
    pallas_call x1, Pallas kernels, on_device(): pl.pallas_call(functools.partial(kernel, n_dp, n_vocab), out_shape=jax.Sh...  39.1 us
    squeeze x1, local copies, waits for them, and re-layouts, on_device(): return (outs[0], outs[1], outs[2])  1.3 us

profile of v4, /device:TPU:0, one launch (start us, length us, event | category | flops | bytes accessed | tf_op | source)
XLA Modules:
  0.0 41.0 jit_solution(8607839920984957418)
XLA Ops:
  0.6 39.1 %shard_map.67 = f32[3,128]{1,0:T(4,128)} custom-call(bf16[128,3584]{1,0:T(8,128)(2,1)} %h_ref.1, bf16[3584,1024]{1,0:T(8,128)(2,1)} %w_ref.1, s32[1,128]{1,0:T(1,128)} %bitcast.8, s32[1,128]{1,0:T(1,128)} %bitcast.9), custom_call_target="tpu_custom_call" | custom-call | tf_op jit(solution)/shard_map/pallas_call | solution.py:311
  39.7 1.3 %slice_bitcast_fusion = (f32[128]{0:T(128)}, f32[128]{0:T(128)}, f32[128]{0:T(128)}) fusion(f32[3,128]{1,0:T(4,128)} %shard_map.67), kind=kLoop, calls=%fused_computation | loop fusion | bytes 3072 | tf_op jit(solution)/shard_map/squeeze | solution.py:339
